TPU v7x, 32 devices: a whole 2x2x4 slice. The times are simulated.
32 devices in a mesh: req: 2 (over core), seq: 16 (over z, y, x).
Axes of the slice: x: 2, y: 2, z: 4, core: 2. Of those that a mesh axis runs over, the one named last changes fastest.
Arguments:
- image_query: bfloat16 [256, 1536], P(('req', 'seq')), parts along dimension 0, may hold values from -6 to 6
- image_key: bfloat16 [256, 1536], P(('req', 'seq')), parts along dimension 0, may hold values from -6 to 6
- image_value: bfloat16 [256, 1536], P(('req', 'seq')), parts along dimension 0, may hold values from -6 to 6
- text_query: bfloat16 [1024, 1536], P('req'), parts along dimension 0, may hold values from -6 to 6
- text_key: bfloat16 [1024, 1536], P('req'), parts along dimension 0, may hold values from -6 to 6
- text_value: bfloat16 [1024, 1536], P('req'), parts along dimension 0, may hold values from -6 to 6
- image_query_gain: float32 [128], replicated, may hold values from 1 to 8
- image_key_gain: float32 [128], replicated, may hold values from 1 to 8
- text_query_gain: float32 [128], replicated, may hold values from 1 to 2.5
- text_key_gain: float32 [128], replicated, may hold values from 1 to 2.5
- image_order: int32 [256], P(('req', 'seq')), parts along dimension 0, may hold values from 0 to 127, each once
- text_length: int32 [2], P('req'), parts along dimension 0, may hold values from 256 to 512
Outputs:
- image_out: bfloat16 [256, 1536], P(('req', 'seq')), parts along dimension 0
- text_out: bfloat16 [1024, 1536], P(('req', 'seq')), parts along dimension 0
There are 2 independent parts, one for each index of `req`. A program takes and returns all parts, laid end to end along the dimension named above; an argument that names none is the same for every part. Nothing has to cross between parts.
Inputs may be any that keep to these rules, and one draw needn't show every extreme that they name: `image_order`: every position 0 to 127 appears once.
All inputs are finite; a program needn't handle non-finite values.
Results may differ from a plain program's by a relative error of at most 0.005.
The roundings to bfloat16 on the way count: a program that leaves them out, or rounds other values in their place, can miss the bound.
Values may be sent and summed in bfloat16 or wider, within the bound.
A program may use at most 64 MiB of HBM per device.

v0:
```python
import jax
import jax.numpy as jnp
from jax import lax
from jax.sharding import PartitionSpec as P

GRID_W = 64


epsilon = 1e-06
masked_score = -1e30


def for_sending(array):

    def short(part):
        return part.astype(jnp.bfloat16) if part.dtype == jnp.float32 else part

    return jax.tree.map(short, array)


def from_partner(block, axis, apart):
    count = lax.axis_size(axis)
    route = []
    for low in range(count):
        high = low | 1 << apart
        if high != low and high < count:
            route += [(low, high), (high, low)]
    return lax.ppermute(block, axis, route)


def shifted(block, axis, distance):
    devices = range(lax.axis_size(axis))
    route = [((i - distance) % len(devices), i) for i in devices]
    return lax.ppermute(block, axis, route)


def head_norm(values, norm_gain, head_count):
    row_count = values.shape[0]
    shaped = values.astype(jnp.float32).reshape(row_count, head_count, -1)
    mean_square = jnp.mean(shaped * shaped, axis=-1, keepdims=True)
    return shaped * lax.rsqrt(mean_square + epsilon) * norm_gain


def rotate(normed, positions, half_length):
    row_count, head_count, head_dim = normed.shape
    pair_count = head_dim // 2
    pair_ids = jnp.arange(pair_count)
    first_axis = pair_ids < 8
    second = pair_ids < 36
    within = jnp.where(first_axis, pair_ids, jnp.where(second, pair_ids - 8, pair_ids - 36)).astype(
        jnp.float32
    )
    axis_dim = jnp.where(first_axis, 16.0, 56.0).astype(jnp.float32)
    frequency = jnp.power(jnp.float32(10000.0), -2.0 * within / axis_dim)
    image_index = positions // half_length
    inside = positions % half_length
    row_place = inside // GRID_W
    column_place = inside % GRID_W
    coordinate = jnp.where(
        first_axis[None, :],
        image_index[:, None],
        jnp.where(second[None, :], row_place[:, None], column_place[:, None]),
    ).astype(jnp.float32)
    angles = coordinate * frequency[None, :]
    cosine = jnp.cos(angles)[:, None, :]
    sine_part = jnp.sin(angles)[:, None, :]
    paired = normed.reshape(row_count, head_count, pair_count, 2)
    even_part = paired[..., 0]
    odd_part = paired[..., 1]
    turned = jnp.stack(
        [even_part * cosine - odd_part * sine_part, even_part * sine_part + odd_part * cosine],
        axis=-1,
    )
    return turned.reshape(row_count, head_count * head_dim)


def partial_attend(queries, key_block, value_block, key_mask, head_count):
    row_count = queries.shape[0]
    key_count = key_block.shape[0]
    query_heads = queries.reshape(row_count, head_count, -1)
    scaling = query_heads.shape[-1] ** (-0.5)
    scores = (
        jnp.einsum(
            "rhd,shd->rhs",
            query_heads,
            key_block.reshape(key_count, head_count, -1),
            preferred_element_type=jnp.float32,
        )
        * scaling
    )
    if key_mask is not None:
        scores = jnp.where(key_mask[None, None, :], scores, masked_score)
    row_max = jnp.max(scores, axis=-1)
    expo = jnp.exp(scores - row_max[..., None])
    if key_mask is not None:
        expo = jnp.where(key_mask[None, None, :], expo, 0.0)
    totals = jnp.sum(expo, axis=-1)
    blended = jnp.einsum(
        "rhs,shd->rhd",
        expo.astype(jnp.bfloat16),
        value_block.reshape(key_count, head_count, -1),
        preferred_element_type=jnp.float32,
    )
    return (row_max, totals, blended)


def combine(earlier, later):
    max_first, sum_first, out_first = earlier
    max_second, sum_second, out_second = later
    joint = jnp.maximum(max_first, max_second)
    factor_first = jnp.exp(max_first - joint)
    factor_second = jnp.exp(max_second - joint)
    return (
        joint,
        sum_first * factor_first + sum_second * factor_second,
        out_first * factor_first[..., None] + out_second * factor_second[..., None],
    )


def finish(state):
    row_max, totals, blended = state
    return (blended / totals[..., None]).reshape(blended.shape[0], -1).astype(jnp.bfloat16)


def spread_groups(block, groups):
    row_count = block.shape[0]
    return block.reshape(row_count, groups, -1).transpose(1, 0, 2)


def regroup(members, place, groups, mover):
    section_count = groups.bit_length() - 1
    for section in range(section_count):
        width = 1 << section
        own_bit = place // width % 2
        shaped = [
            member.reshape((member.shape[0] // (2 * width), 2, width) + member.shape[1:])
            for member in members
        ]
        outgoing = tuple(
            (lax.dynamic_index_in_dim(piece, 1 - own_bit, 1, keepdims=False) for piece in shaped)
        )
        kept = [lax.dynamic_index_in_dim(piece, own_bit, 1, keepdims=False) for piece in shaped]
        received = mover(outgoing, section)
        rebuilt = []
        for index in range(len(members)):
            lower = jnp.where(own_bit == 0, kept[index], received[index])
            upper = jnp.where(own_bit == 0, received[index], kept[index])
            rebuilt.append(jnp.stack([lower, upper], axis=1).reshape(members[index].shape))
        members = tuple(rebuilt)
    return members


def local(
    image_query,
    image_key,
    image_value,
    text_query,
    text_key,
    text_value,
    image_query_gain,
    image_key_gain,
    text_query_gain,
    text_key_gain,
    image_order,
    text_length,
):
    head_size = image_query_gain.shape[0]
    head_count = image_query.shape[1] // head_size
    devices = lax.axis_size("seq")
    own_rows = image_query.shape[0]
    half_length = own_rows * devices // 2
    text_rows = text_query.shape[0]
    share = text_rows // devices
    first_row = lax.axis_index("seq") * share
    query_ready = rotate(
        head_norm(image_query, image_query_gain, head_count), image_order, half_length
    ).astype(jnp.bfloat16)
    key_ready = rotate(
        head_norm(image_key, image_key_gain, head_count), image_order, half_length
    ).astype(jnp.bfloat16)
    text_valid = jnp.arange(text_rows) < text_length[0]
    groups = 4
    place = lax.axis_index("seq") % groups
    group_heads = head_count // groups
    span = group_heads * head_size
    own_text = lax.dynamic_slice_in_dim(text_query, first_row, share, 0)
    own_ready = (
        head_norm(own_text, text_query_gain, head_count).reshape(share, -1).astype(jnp.bfloat16)
    )
    local_queries = jnp.concatenate([query_ready, own_ready], axis=0)
    query_count = local_queries.shape[0]

    def forward_move(parts, section):
        return jax.tree.map(
            lambda part, own: part.astype(own.dtype),
            from_partner(for_sending(parts), "seq", section),
            parts,
        )

    moved = regroup(
        (
            spread_groups(local_queries, groups),
            spread_groups(key_ready, groups),
            spread_groups(image_value, groups),
        ),
        place,
        groups,
        forward_move,
    )
    queries_here = moved[0].reshape(-1, span)
    keys_here = moved[1].reshape(-1, span)
    values_here = moved[2].reshape(-1, span)
    text_key_part = lax.dynamic_slice_in_dim(text_key, place * span, span, 1)
    text_value_part = lax.dynamic_slice_in_dim(text_value, place * span, span, 1)
    text_keys_here = (
        head_norm(text_key_part, text_key_gain, group_heads)
        .reshape(text_rows, -1)
        .astype(jnp.bfloat16)
    )
    state = combine(
        partial_attend(queries_here, text_keys_here, text_value_part, text_valid, group_heads),
        partial_attend(queries_here, keys_here, values_here, None, group_heads),
    )

    def one_turn(step, carry):
        current, keys_now, values_now = carry
        keys_now, values_now = shifted((keys_now, values_now), "seq", groups)
        current = combine(
            current, partial_attend(queries_here, keys_now, values_now, None, group_heads)
        )
        return (current, keys_now, values_now)

    looped = lax.fori_loop(0, devices // groups - 1, one_turn, (state, keys_here, values_here))
    outputs = finish(looped[0]).reshape(groups, query_count, span)

    def backward_move(parts, section):
        return jax.tree.map(
            lambda part, own: part.astype(own.dtype),
            from_partner(for_sending(parts), "seq", section),
            parts,
        )

    returned = regroup((outputs,), place, groups, backward_move)[0]
    rows_back = returned.transpose(1, 0, 2).reshape(query_count, head_count * head_size)
    return (rows_back[:own_rows], rows_back[own_rows:])


def solution(mesh):
    placed = (
        P(("req", "seq"), None),
        P(("req", "seq"), None),
        P(("req", "seq"), None),
        P("req", None),
        P("req", None),
        P("req", None),
        P(),
        P(),
        P(),
        P(),
        P(("req", "seq")),
        P("req"),
    )
    return jax.shard_map(
        local,
        mesh=mesh,
        in_specs=placed,
        out_specs=(P(("req", "seq"), None), P(("req", "seq"), None)),
        check_vma=False,
    )
```

profile of v0, /device:TPU:0, one launch (start us, length us, event | category | flops | bytes accessed | tf_op | source)
XLA Modules:
  0.0 64.9 jit_solution(8278273655479829791)
XLA Ops:
  0.8 0.9 %copy.129 = f32[8,1536]{0,1:T(8,128)S(1)} copy(bf16[8,1536]{1,0:T(8,128)(2,1)} %param.15) | data formatting | bytes 73728 | tf_op jit(solution)/shard_map/convert_element_type | solution.py:39
  1.7 0.8 %bitcast_reduce_fusion = f32[8,12]{0,1:T(8,128)S(1)} fusion(bf16[8,1536]{1,0:T(8,128)(2,1)} %param.15), kind=kLoop, calls=%fused_computation.93 | loop fusion | flops 36768 | bytes 24960 | tf_op jit(solution)/shard_map/reduce_sum | solution.py:40
  2.5 0.9 %copy.116 = f32[8,1536]{0,1:T(8,128)S(1)} copy(bf16[8,1536]{1,0:T(8,128)(2,1)} %param.14) | data formatting | bytes 73728 | tf_op jit(solution)/shard_map/convert_element_type | solution.py:39
  4.2 0.9 %multiply_multiply_fusion = (f32[8,12,64,2]{0,3,2,1:T(2,128)S(1)}, f32[8,12,64,2]{0,3,2,1:T(2,128)S(1)}) fusion(f32[8,12,64,2]{0,3,2,1:T(2,128)S(1)} %bitcast.205, f32[64,2]{1,0:T(8,128)S(1)} %mul.311, f32[8,12]{0,1:T(8,128)S(1)} %add_rsqrt_fusion.1, f32[64,2]{1,0:T(8,128)S(1)} %mul.283, f32[8,12,64,2]{0,3,2,1:T(2,128)S(1)} %bitcast.206, ...), kind=kLoop, calls=%fused_computation.34 | loop fusion | flops 49152 | bytes 198400 | tf_op jit(solution)/shard_map/mul | solution.py:41
  5.1 3.2 %slice_multiply_fusion.5 = (f32[8,12,64,1]{0,3,2,1:T(1,128)S(1)}, f32[8,12,64,1]{0,3,2,1:T(1,128)S(1)}, f32[8,12,64,1]{0,3,2,1:T(1,128)S(1)}, f32[8,12,64,1]{0,3...) fusion(f32[8,12,64,2]{0,3,2,1:T(2,128)S(1)} %get-tuple-element., ...), kind=kLoop, calls=%fused_computation.47 | loop fusion | flops 49152 | bytes 299008 | tf_op jit(solution)/shard_map/mul | solution.py:71
  9.8 0.9 %convert_multiply_fusion.3 = f32[32,1536]{1,0:T(8,128)S(1)} fusion(bf16[512,1536]{1,0:T(8,128)(2,1)} %param.17, s32[]{:T(128)S(6)} %select_n.241), kind=kLoop, calls=%fused_computation.41 | loop fusion | flops 98304 | bytes 294916 | tf_op jit(solution)/shard_map/mul | solution.py:40
  11.1 1.0 %fusion.27 = bf16[32,1536]{1,0:T(8,128)(2,1)S(1)} fusion(f32[4,8,12,128]{3,2,1,0:T(8,128)S(1)} %bitcast.211, f32[1536]{0:T(1024)S(1)} %broadcast_bitcast_fusion, bf16[512,1536]{1,0:T(8,128)(2,1)} %param.17, s32[]{:T(128)S(6)} %select_n.241), kind=kLoop, calls=%fused_computation.51 | loop fusion | flops 196608 | bytes 399364 | tf_op jit(solution)/shard_map/convert_element_type | solution.py:188
  12.5 3.0 %collective-permute-start.2 = (bf16[2,1,40,384]{3,2,0,1:T(8,128)(2,1)S(1)}, bf16[2,1,40,384]{3,2,0,1:T(8,128)(2,1)S(1)}, u32[]{:S(2)}, u32[]{:S(2)}) collective-permute-start(bf16[2,1,40,384]{3,2,0,1:T(8,128)(2,1)S(1)} %bitcast.219), channel_id=1, source_target_pairs={{0,1},{1,0},{2,3},{3,2},{4,5},{5,4},{6,7},{7,6},{8,9},{9,8},{10,11... | collective-permute-start | bytes 184328 | tf_op jit(solution)/shard_map/ppermute | solution.py:28
  17.2 2.0 %collective-permute-start.6 = (bf16[2,1,8,384]{3,2,0,1:T(8,128)(2,1)S(1)}, bf16[2,1,8,384]{3,2,0,1:T(8,128)(2,1)S(1)}, u32[]{:S(2)}, u32[]{:S(2)}) collective-permute-start(bf16[2,1,8,384]{3,2,0,1:T(8,128)(2,1)S(1)} %dynamic-slice_bitcast_fusion.1), channel_id=1, source_target_pairs={{0,1},{1,0},{2,3},{3,2},{4,5},{5,4},{6,7},{7,6},{8,9},{9,8},{10,11... | collective-permute-start | bytes 36872 | tf_op jit(solution)/shard_map/ppermute | solution.py:28
  19.2 1.2 %constant_dynamic-slice_fusion = (bf16[512,384]{1,0:T(8,128)(2,1)S(1)}, bf16[512,384]{1,0:T(8,128)(2,1)S(1)}) fusion(bf16[512,1536]{1,0:T(8,128)(2,1)} %param.19, s32[]{:T(128)S(6)} %select_n.231, bf16[512,1536]{1,0:T(8,128)(2,1)} %param.18), kind=kLoop, calls=%fused_computation.138 | loop fusion | bytes 1572868 | tf_op jit(solution)/shard_map/dynamic_slice | solution.py:214
  22.3 1.6 %collective-permute-start.5 = (bf16[1,2,8,384]{3,2,1,0:T(8,128)(2,1)S(1)}, bf16[1,2,8,384]{3,2,1,0:T(8,128)(2,1)S(1)}, u32[]{:S(2)}, u32[]{:S(2)}) collective-permute-start(bf16[1,2,8,384]{3,2,1,0:T(8,128)(2,1)S(1)} %fusion.53), channel_id=1, source_target_pairs={{0,2},{2,0},{1,3},{3,1},{4,6},{6,4},{5,7},{7,5},{8,10},{10,8},{9,1... | collective-permute-start | bytes 36872 | tf_op jit(solution)/shard_map/ppermute | solution.py:28
  23.9 0.6 collective-permute-start.7
  24.5 1.6 %collective-permute-done.5 = bf16[1,2,8,384]{3,2,1,0:T(8,128)(2,1)S(1)} collective-permute-done((bf16[1,2,8,384]{3,2,1,0:T(8,128)(2,1)S(1)}, bf16[1,2,8,384]{3,2,1,0:T(8,128)(2,1)S(1)}, u32[]{:S(2)}, u32[]{:S(2)}) %collective-permute-start.5) | collective-permute-done | bytes 12320 | tf_op jit(solution)/shard_map/ppermute | solution.py:28
  26.1 1.6 %collective-permute-done.7 = bf16[1,2,8,384]{3,2,1,0:T(8,128)(2,1)S(1)} collective-permute-done((bf16[1,2,8,384]{3,2,1,0:T(8,128)(2,1)S(1)}, bf16[1,2,8,384]{3,2,1,0:T(8,128)(2,1)S(1)}, u32[]{:S(2)}, u32[]{:S(2)}) %collective-permute-start.7) | collective-permute-done | bytes 12320 | tf_op jit(solution)/shard_map/ppermute | solution.py:28
  27.8 0.6 collective-permute-start.3
  28.4 3.7 %collective-permute-done.3 = bf16[1,2,40,384]{3,2,1,0:T(8,128)(2,1)S(1)} collective-permute-done((bf16[1,2,40,384]{3,2,1,0:T(8,128)(2,1)S(1)}, bf16[1,2,40,384]{3,2,1,0:T(8,128)(2,1)S(1)}, u32[]{:S(2)}, u32[]{:S(2)}) %collective-permute-start.3) | collective-permute-done | bytes 61472 | tf_op jit(solution)/shard_map/ppermute | solution.py:28
  33.5 0.4 fusion.15
  33.9 20.5 %while.18 = (s32[]{:T(128)}, f32[160,3]{0,1:T(4,128)S(1)}, f32[160,3]{0,1:T(4,128)S(1)}, f32[160,3,128]{2,0,1:T(8,128)S(1)}, bf16[32,384]{1,0:T(8,128)(2,1)S(1)}...) while((s32[]{:T(128)}, f32[160,3]{0,1:T(4,128)S(1)}, ...), condition=%wide.region_11.12_spmd, body=%wide.region_8.11_spmd.sunk | while | flops 8142722 | bytes 1415589 | solution.py:233
  33.9 1.6 %collective-permute-start = (bf16[32,384]{1,0:T(8,128)(2,1)S(1)}, bf16[32,384]{1,0:T(8,128)(2,1)S(1)}, u32[]{:S(2)}, u32[]{:S(2)}) collective-permute-start(bf16[32,384]{1,0:T(8,128)(2,1)S(1)} %get-tuple-element.185), channel_id=1, source_target_pairs={{12,0},{13,1},{14,2},{15,3},{0,4},{1,5},{2,6},{3,7},{4,8},{5,9},{6... | collective-permute-start | bytes 73736 | tf_op jit(solution)/shard_map/while/body/eval_jaxpr/ppermute | solution.py:34
  35.6 1.6 %collective-permute-start.1 = (bf16[32,384]{1,0:T(8,128)(2,1)S(1)}, bf16[32,384]{1,0:T(8,128)(2,1)S(1)}, u32[]{:S(2)}, u32[]{:S(2)}) collective-permute-start(bf16[32,384]{1,0:T(8,128)(2,1)S(1)} %get-tuple-element.186), channel_id=1, source_target_pairs={{12,0},{13,1},{14,2},{15,3},{0,4},{1,5},{2,6},{3,7},{4,8},{5,9},{6... | collective-permute-start | bytes 73736 | tf_op jit(solution)/shard_map/while/body/eval_jaxpr/ppermute | solution.py:34
  37.2 2.4 %collective-permute-done = bf16[32,384]{1,0:T(8,128)(2,1)S(1)} collective-permute-done((bf16[32,384]{1,0:T(8,128)(2,1)S(1)}, bf16[32,384]{1,0:T(8,128)(2,1)S(1)}, u32[]{:S(2)}, u32[]{:S(2)}) %collective-permute-start) | collective-permute-done | bytes 24608 | tf_op jit(solution)/shard_map/while/body/eval_jaxpr/ppermute | solution.py:34
  39.9 1.5 %collective-permute-done.1 = bf16[32,384]{1,0:T(8,128)(2,1)S(1)} collective-permute-done((bf16[32,384]{1,0:T(8,128)(2,1)S(1)}, bf16[32,384]{1,0:T(8,128)(2,1)S(1)}, u32[]{:S(2)}, u32[]{:S(2)}) %collective-permute-start.1) | collective-permute-done | bytes 24608 | tf_op jit(solution)/shard_map/while/body/eval_jaxpr/ppermute | solution.py:34
  41.8 1.1 %collective-permute-start.1 = (bf16[32,384]{1,0:T(8,128)(2,1)S(1)}, bf16[32,384]{1,0:T(8,128)(2,1)S(1)}, u32[]{:S(2)}, u32[]{:S(2)}) collective-permute-start(bf16[32,384]{1,0:T(8,128)(2,1)S(1)} %get-tuple-element.186), channel_id=1, source_target_pairs={{12,0},{13,1},{14,2},{15,3},{0,4},{1,5},{2,6},{3,7},{4,8},{5,9},{6... | collective-permute-start | bytes 73736 | tf_op jit(solution)/shard_map/while/body/eval_jaxpr/ppermute | solution.py:34
  43.0 4.4 %collective-permute-done = bf16[32,384]{1,0:T(8,128)(2,1)S(1)} collective-permute-done((bf16[32,384]{1,0:T(8,128)(2,1)S(1)}, bf16[32,384]{1,0:T(8,128)(2,1)S(1)}, u32[]{:S(2)}, u32[]{:S(2)}) %collective-permute-start) | collective-permute-done | bytes 24608 | tf_op jit(solution)/shard_map/while/body/eval_jaxpr/ppermute | solution.py:34
  48.2 0.5 collective-permute-start.1
  48.7 5.1 %collective-permute-done = bf16[32,384]{1,0:T(8,128)(2,1)S(1)} collective-permute-done((bf16[32,384]{1,0:T(8,128)(2,1)S(1)}, bf16[32,384]{1,0:T(8,128)(2,1)S(1)}, u32[]{:S(2)}, u32[]{:S(2)}) %collective-permute-start) | collective-permute-done | bytes 24608 | tf_op jit(solution)/shard_map/while/body/eval_jaxpr/ppermute | solution.py:34
  54.8 0.6 collective-permute-start.8
  55.4 3.7 %collective-permute-done.8 = bf16[2,1,40,384]{3,2,0,1:T(8,128)(2,1)S(1)} collective-permute-done((bf16[2,1,40,384]{3,2,0,1:T(8,128)(2,1)S(1)}, bf16[2,1,40,384]{3,2,0,1:T(8,128)(2,1)S(1)}, u32[]{:S(2)}, u32[]{:S(2)}) %collective-permute-start.8) | collective-permute-done | bytes 61472 | tf_op jit(solution)/shard_map/ppermute | solution.py:28
  59.2 0.6 collective-permute-start.9
  59.7 3.7 %collective-permute-done.9 = bf16[1,2,40,384]{3,2,1,0:T(8,128)(2,1)S(1)} collective-permute-done((bf16[1,2,40,384]{3,2,1,0:T(8,128)(2,1)S(1)}, bf16[1,2,40,384]{3,2,1,0:T(8,128)(2,1)S(1)}, u32[]{:S(2)}, u32[]{:S(2)}) %collective-permute-start.9) | collective-permute-done | bytes 61472 | tf_op jit(solution)/shard_map/ppermute | solution.py:28
  63.6 0.7 %copy.154 = bf16[4,8,4,384]{3,1,2,0:T(8,128)(2,1)} copy(bf16[4,8,4,384]{3,2,1,0:T(4,128)(2,1)S(1)} %bitcast.215) | data formatting | bytes 196608
  64.3 0.6 copy.153
  (127 shorter events, 9.9 us)
Async XLA Ops:
  0.6 10.3 %copy-start = (f32[128]{0:T(128)S(1)}, f32[128]{0:T(128)}, u32[]{:S(2)}) copy-start(f32[128]{0:T(128)} %param.22) | copy-start | bytes 1540
  0.6 2.8 %copy-start.1 = (bf16[8,1536]{1,0:T(8,128)(2,1)S(1)}, bf16[8,1536]{1,0:T(8,128)(2,1)}, u32[]{:S(2)}) copy-start(bf16[8,1536]{1,0:T(8,128)(2,1)} %param.14) | copy-start | bytes 73732
  0.7 2.8 %copy-start.6 = (s32[8]{0:T(128)S(1)}, s32[8]{0:T(128)}, u32[]{:S(2)}) copy-start(s32[8]{0:T(128)} %param.24) | copy-start | bytes 100
  0.7 3.2 %copy-start.3 = (f32[128]{0:T(128)S(1)}, f32[128]{0:T(128)}, u32[]{:S(2)}) copy-start(f32[128]{0:T(128)} %param.20) | copy-start | bytes 1540
  0.7 3.3 %copy-start.4 = (f32[128]{0:T(128)S(1)}, f32[128]{0:T(128)}, u32[]{:S(2)}) copy-start(f32[128]{0:T(128)} %param.21) | copy-start | bytes 1540
  12.5 15.2 %collective-permute-start.2 = (bf16[2,1,40,384]{3,2,0,1:T(8,128)(2,1)S(1)}, bf16[2,1,40,384]{3,2,0,1:T(8,128)(2,1)S(1)}, u32[]{:S(2)}, u32[]{:S(2)}) collective-permute-start(bf16[2,1,40,384]{3,2,0,1:T(8,128)(2,1)S(1)} %bitcast.219), channel_id=1, source_target_pairs={{0,1},{1,0},{2,3},{3,2},{4,5},{5,4},{6,7},{7,6},{8,9},{9,8},{10,11... | collective-permute-start | bytes 184328 | tf_op jit(solution)/shard_map/ppermute | solution.py:28
  15.8 1.4 %copy-start.2 = (bf16[8,1536]{1,0:T(8,128)(2,1)S(1)}, bf16[8,1536]{1,0:T(8,128)(2,1)}, u32[]{:S(2)}) copy-start(bf16[8,1536]{1,0:T(8,128)(2,1)} %param.16) | copy-start | bytes 73732
  17.1 5.1 %collective-permute-start.4 = (bf16[2,1,8,384]{3,2,0,1:T(8,128)(2,1)S(1)}, bf16[2,1,8,384]{3,2,0,1:T(8,128)(2,1)S(1)}, u32[]{:S(2)}, u32[]{:S(2)}) collective-permute-start(bf16[2,1,8,384]{3,2,0,1:T(8,128)(2,1)S(1)} %bitcast.223), channel_id=1, source_target_pairs={{0,1},{1,0},{2,3},{3,2},{4,5},{5,4},{6,7},{7,6},{8,9},{9,8},{10,11... | collective-permute-start | bytes 36872 | tf_op jit(solution)/shard_map/ppermute | solution.py:28
  17.2 6.7 %collective-permute-start.6 = (bf16[2,1,8,384]{3,2,0,1:T(8,128)(2,1)S(1)}, bf16[2,1,8,384]{3,2,0,1:T(8,128)(2,1)S(1)}, u32[]{:S(2)}, u32[]{:S(2)}) collective-permute-start(bf16[2,1,8,384]{3,2,0,1:T(8,128)(2,1)S(1)} %dynamic-slice_bitcast_fusion.1), channel_id=1, source_target_pairs={{0,1},{1,0},{2,3},{3,2},{4,5},{5,4},{6,7},{7,6},{8,9},{9,8},{10,11... | collective-permute-start | bytes 36872 | tf_op jit(solution)/shard_map/ppermute | solution.py:28
  20.4 0.7 %copy-start.5 = (f32[128]{0:T(128)S(1)}, f32[128]{0:T(128)}, u32[]{:S(2)}) copy-start(f32[128]{0:T(128)} %param.23) | copy-start | bytes 1540
  22.3 3.8 %collective-permute-start.5 = (bf16[1,2,8,384]{3,2,1,0:T(8,128)(2,1)S(1)}, bf16[1,2,8,384]{3,2,1,0:T(8,128)(2,1)S(1)}, u32[]{:S(2)}, u32[]{:S(2)}) collective-permute-start(bf16[1,2,8,384]{3,2,1,0:T(8,128)(2,1)S(1)} %fusion.53), channel_id=1, source_target_pairs={{0,2},{2,0},{1,3},{3,1},{4,6},{6,4},{5,7},{7,5},{8,10},{10,8},{9,1... | collective-permute-start | bytes 36872 | tf_op jit(solution)/shard_map/ppermute | solution.py:28
  23.9 3.8 %collective-permute-start.7 = (bf16[1,2,8,384]{3,2,1,0:T(8,128)(2,1)S(1)}, bf16[1,2,8,384]{3,2,1,0:T(8,128)(2,1)S(1)}, u32[]{:S(2)}, u32[]{:S(2)}) collective-permute-start(bf16[1,2,8,384]{3,2,1,0:T(8,128)(2,1)S(1)} %fusion.49), channel_id=1, source_target_pairs={{0,2},{2,0},{1,3},{3,1},{4,6},{6,4},{5,7},{7,5},{8,10},{10,8},{9,1... | collective-permute-start | bytes 36872 | tf_op jit(solution)/shard_map/ppermute | solution.py:28
  27.8 4.3 %collective-permute-start.3 = (bf16[1,2,40,384]{3,2,1,0:T(8,128)(2,1)S(1)}, bf16[1,2,40,384]{3,2,1,0:T(8,128)(2,1)S(1)}, u32[]{:S(2)}, u32[]{:S(2)}) collective-permute-start(bf16[1,2,40,384]{3,2,1,0:T(8,128)(2,1)S(1)} %fusion.37), channel_id=1, source_target_pairs={{0,2},{2,0},{1,3},{3,1},{4,6},{6,4},{5,7},{7,5},{8,10},{10,8},{9,1... | collective-permute-start | bytes 184328 | tf_op jit(solution)/shard_map/ppermute | solution.py:28
  33.9 5.7 %collective-permute-start = (bf16[32,384]{1,0:T(8,128)(2,1)S(1)}, bf16[32,384]{1,0:T(8,128)(2,1)S(1)}, u32[]{:S(2)}, u32[]{:S(2)}) collective-permute-start(bf16[32,384]{1,0:T(8,128)(2,1)S(1)} %get-tuple-element.185), channel_id=1, source_target_pairs={{12,0},{13,1},{14,2},{15,3},{0,4},{1,5},{2,6},{3,7},{4,8},{5,9},{6... | collective-permute-start | bytes 73736 | tf_op jit(solution)/shard_map/while/body/eval_jaxpr/ppermute | solution.py:34
  35.6 5.8 %collective-permute-start.1 = (bf16[32,384]{1,0:T(8,128)(2,1)S(1)}, bf16[32,384]{1,0:T(8,128)(2,1)S(1)}, u32[]{:S(2)}, u32[]{:S(2)}) collective-permute-start(bf16[32,384]{1,0:T(8,128)(2,1)S(1)} %get-tuple-element.186), channel_id=1, source_target_pairs={{12,0},{13,1},{14,2},{15,3},{0,4},{1,5},{2,6},{3,7},{4,8},{5,9},{6... | collective-permute-start | bytes 73736 | tf_op jit(solution)/shard_map/while/body/eval_jaxpr/ppermute | solution.py:34
  41.8 5.7 %collective-permute-start = (bf16[32,384]{1,0:T(8,128)(2,1)S(1)}, bf16[32,384]{1,0:T(8,128)(2,1)S(1)}, u32[]{:S(2)}, u32[]{:S(2)}) collective-permute-start(bf16[32,384]{1,0:T(8,128)(2,1)S(1)} %get-tuple-element.185), channel_id=1, source_target_pairs={{12,0},{13,1},{14,2},{15,3},{0,4},{1,5},{2,6},{3,7},{4,8},{5,9},{6... | collective-permute-start | bytes 73736 | tf_op jit(solution)/shard_map/while/body/eval_jaxpr/ppermute | solution.py:34
  41.8 5.9 %collective-permute-start.1 = (bf16[32,384]{1,0:T(8,128)(2,1)S(1)}, bf16[32,384]{1,0:T(8,128)(2,1)S(1)}, u32[]{:S(2)}, u32[]{:S(2)}) collective-permute-start(bf16[32,384]{1,0:T(8,128)(2,1)S(1)} %get-tuple-element.186), channel_id=1, source_target_pairs={{12,0},{13,1},{14,2},{15,3},{0,4},{1,5},{2,6},{3,7},{4,8},{5,9},{6... | collective-permute-start | bytes 73736 | tf_op jit(solution)/shard_map/while/body/eval_jaxpr/ppermute | solution.py:34
  48.1 5.7 %collective-permute-start = (bf16[32,384]{1,0:T(8,128)(2,1)S(1)}, bf16[32,384]{1,0:T(8,128)(2,1)S(1)}, u32[]{:S(2)}, u32[]{:S(2)}) collective-permute-start(bf16[32,384]{1,0:T(8,128)(2,1)S(1)} %get-tuple-element.185), channel_id=1, source_target_pairs={{12,0},{13,1},{14,2},{15,3},{0,4},{1,5},{2,6},{3,7},{4,8},{5,9},{6... | collective-permute-start | bytes 73736 | tf_op jit(solution)/shard_map/while/body/eval_jaxpr/ppermute | solution.py:34
  48.2 5.9 %collective-permute-start.1 = (bf16[32,384]{1,0:T(8,128)(2,1)S(1)}, bf16[32,384]{1,0:T(8,128)(2,1)S(1)}, u32[]{:S(2)}, u32[]{:S(2)}) collective-permute-start(bf16[32,384]{1,0:T(8,128)(2,1)S(1)} %get-tuple-element.186), channel_id=1, source_target_pairs={{12,0},{13,1},{14,2},{15,3},{0,4},{1,5},{2,6},{3,7},{4,8},{5,9},{6... | collective-permute-start | bytes 73736 | tf_op jit(solution)/shard_map/while/body/eval_jaxpr/ppermute | solution.py:34
  54.8 4.3 %collective-permute-start.8 = (bf16[2,1,40,384]{3,2,0,1:T(8,128)(2,1)S(1)}, bf16[2,1,40,384]{3,2,0,1:T(8,128)(2,1)S(1)}, u32[]{:S(2)}, u32[]{:S(2)}) collective-permute-start(bf16[2,1,40,384]{3,2,0,1:T(8,128)(2,1)S(1)} %dynamic-slice_bitcast_fusion), channel_id=1, source_target_pairs={{0,1},{1,0},{2,3},{3,2},{4,5},{5,4},{6,7},{7,6},{8,9},{9,8},{10,11... | collective-permute-start | bytes 184328 | tf_op jit(solution)/shard_map/ppermute | solution.py:28
  59.2 4.3 %collective-permute-start.9 = (bf16[1,2,40,384]{3,2,1,0:T(8,128)(2,1)S(1)}, bf16[1,2,40,384]{3,2,1,0:T(8,128)(2,1)S(1)}, u32[]{:S(2)}, u32[]{:S(2)}) collective-permute-start(bf16[1,2,40,384]{3,2,1,0:T(8,128)(2,1)S(1)} %fusion.33), channel_id=1, source_target_pairs={{0,2},{2,0},{1,3},{3,1},{4,6},{6,4},{5,7},{7,5},{8,10},{10,8},{9,1... | collective-permute-start | bytes 184328 | tf_op jit(solution)/shard_map/ppermute | solution.py:28
where the time goes:
time: 65.3 us; the launch traced here: 64.9 us
  waiting for transfers between devices  27.7 us (42%)
  starting transfers between devices  14 us (21%)
  local copies, waits for them, and re-layouts  9.5 us (15%)
  other arithmetic  8.71 us (13%)
  matrix products  2.9 us (4%)
  between operations  1.97 us (3%)
    ppermute x8, waiting for transfers between devices, from_partner(): return lax.ppermute(block, axis, route)  14.3 us
    ppermute x6, waiting for transfers between devices, shifted(): return lax.ppermute(block, axis, route)  13.4 us
    ppermute x8, starting transfers between devices, from_partner(): return lax.ppermute(block, axis, route)  9 us
    ppermute x6, starting transfers between devices, shifted(): return lax.ppermute(block, axis, route)  4.97 us
    mul x1, other arithmetic, rotate(): odd_part * sine_part  3.16 us
    unnamed x21, local copies, waits for them, and re-layouts  2.18 us
    convert_element_type x2, local copies, waits for them, and re-layouts, head_norm(): shaped = values.astype(jnp.float32).reshape(row_count, head_count, -1)  1.81 us
    dot_general x5, matrix products, partial_attend(): jnp.einsum('rhs,shd->rhd', expo.astype(jnp.bfloat16), value_block.reshape...  1.64 us
  transfers between devices with their start and end apart: 14, of which 9 were waited for; matrix products, arithmetic and copies ran while one was open for 7% of the time, Pallas kernels for 0%

commit v1 on v0

v1 whole, which is shorter than its diff:
```python
import functools
import math

import jax
import jax.numpy as jnp
from jax import lax
from jax.experimental import pallas as pl
from jax.experimental.pallas import tpu as pltpu
from jax.sharding import PartitionSpec as P

GRID_W = 64
EPS = 1e-06
LOW = -1e30
MESH = pl.DeviceIdType.MESH


def line_sizes(devices):
    z_size = 4 if devices % 4 == 0 else 1
    rest = devices // z_size
    x_size = 1
    while x_size * x_size * 4 <= rest and rest % (x_size * 2) == 0:
        x_size *= 2
    return z_size, rest // x_size, x_size


def rsqrt_mean(values):
    return lax.rsqrt(jnp.mean(values * values, axis=-1, keepdims=True) + EPS)


def kernel(
    devices,
    iq_ref,
    ik_ref,
    iv_ref,
    tq_ref,
    tk_ref,
    tv_ref,
    iqg_ref,
    ikg_ref,
    tqg_ref,
    tkg_ref,
    order_ref,
    length_ref,
    io_ref,
    to_ref,
    kbuf,
    vbuf,
    tq_buf,
    tk_buf,
    tv_buf,
    qs,
    m_buf,
    l_buf,
    o_buf,
    recv_sem,
    send_sem,
    local_sem,
):
    zs, ys, xs = line_sizes(devices)
    me = lax.axis_index("seq")
    req = lax.axis_index("req")
    x_me = me % xs
    y_me = (me // xs) % ys
    z_me = me // (xs * ys)

    def block(z, y, x):
        return (z * ys + y) * xs + x

    if zs == 4:
        z_others = [z_me + 1 - 2 * (z_me % 2), 3 - z_me, (z_me + 2) % 4]
    else:
        z_others = []
    y_others = [(y_me + d) % ys for d in range(1, ys)]
    x_others = [(x_me + d) % xs for d in range(1, xs)]
    z_peers = [block(z, y_me, x_me) for z in z_others]
    y_peers = [block(z_me, y, x_me) for y in y_others]
    x_peers = [block(z_me, y_me, x) for x in x_others]
    peers = z_peers + y_peers + x_peers

    barrier = pltpu.get_barrier_semaphore()
    for peer in peers:
        pl.semaphore_signal(barrier, inc=1, device_id=(req, peer), device_id_type=MESH)

    own_rows, width = iq_ref.shape
    size = iqg_ref.shape[-1]
    heads = width // size
    share = tq_buf.shape[0]
    text_rows = tk_ref.shape[0]
    rows = share + own_rows
    groups = tk_buf.shape[0]
    per = heads // groups
    span = per * size
    scale = math.log2(math.e) / math.sqrt(size)

    tq_copy = pltpu.make_async_copy(
        tq_ref.at[pl.ds(pl.multiple_of(me * share, share), share), :],
        tq_buf,
        local_sem.at[2 * groups],
    )
    tq_copy.start()
    text_copies = []
    for g in range(groups):
        pair = (
            pltpu.make_async_copy(
                tk_ref.at[:, pl.ds(g * span, span)], tk_buf.at[g], local_sem.at[2 * g]
            ),
            pltpu.make_async_copy(
                tv_ref.at[:, pl.ds(g * span, span)], tv_buf.at[g], local_sem.at[2 * g + 1]
            ),
        )
        for copy in pair:
            copy.start()
        text_copies.append(pair)

    half_length = own_rows * devices // 2
    lane = lax.broadcasted_iota(jnp.int32, (own_rows, size), 1)
    row = lax.broadcasted_iota(jnp.int32, (own_rows, size), 0)
    pair_id = lane // 2
    first = pair_id < 8
    second = pair_id < 36
    coordinate = jnp.zeros((own_rows, size), jnp.int32)
    for r in range(own_rows):
        position = order_ref[r]
        inside = position % half_length
        here = jnp.where(
            first,
            position // half_length,
            jnp.where(second, inside // GRID_W, inside % GRID_W),
        )
        coordinate = jnp.where(row == r, here, coordinate)
    within = jnp.where(first, pair_id, jnp.where(second, pair_id - 8, pair_id - 36))
    step = jnp.where(first, 2.0 / 16.0, 2.0 / 56.0) * (-math.log(10000.0))
    angle = coordinate.astype(jnp.float32) * jnp.exp(within.astype(jnp.float32) * step)
    cosine = jnp.cos(angle)
    sine = jnp.sin(angle)
    even = lane % 2 == 0
    sine = jnp.where(even, -sine, sine)

    def turned(values, gain):
        normed = values * rsqrt_mean(values) * gain
        swapped = jnp.where(
            even, pltpu.roll(normed, size - 1, 1), pltpu.roll(normed, 1, 1)
        )
        return normed * cosine + swapped * sine

    for h in range(heads):
        cols = slice(h * size, (h + 1) * size)
        key = turned(ik_ref[:, cols].astype(jnp.float32), ikg_ref[...])
        kbuf[me, :, cols] = key.astype(jnp.bfloat16)
    vbuf[me] = iv_ref[...]

    pl.semaphore_wait(barrier, len(peers))

    count = [0]
    sends = []

    def send(kind, idx, peer, source=None):
        buf = (kbuf, vbuf)[kind]
        copy = pltpu.make_async_remote_copy(
            src_ref=buf.at[idx] if source is None else source,
            dst_ref=buf.at[idx],
            send_sem=send_sem.at[count[0]],
            recv_sem=recv_sem.at[kind, idx],
            device_id=(req, peer),
            device_id_type=MESH,
        )
        count[0] += 1
        copy.start()
        sends.append(copy)

    def arrive(kind, idx):
        buf = (kbuf, vbuf)[kind]
        pltpu.make_async_remote_copy(
            src_ref=buf.at[idx],
            dst_ref=buf.at[idx],
            send_sem=send_sem.at[0],
            recv_sem=recv_sem.at[kind, idx],
            device_id=(req, me),
            device_id_type=MESH,
        ).wait_recv()

    for group in (z_peers, y_peers, x_peers):
        for peer in group:
            send(1, me, peer, iv_ref)
            send(0, me, peer)

    def near_plane():
        for y in y_others:
            idx = block(z_me, y, x_me)
            arrive(0, idx)
            for peer in x_peers:
                send(0, idx, peer)
        for x in x_others:
            idx = block(z_me, y_me, x)
            arrive(1, idx)
            for peer in y_peers:
                send(1, idx, peer)

    def far_column(z):
        idx = block(z, y_me, x_me)
        for kind in (0, 1):
            arrive(kind, idx)
            for peer in y_peers + x_peers:
                send(kind, idx, peer)

    def far_plane(z):
        for y in y_others:
            idx = block(z, y, x_me)
            arrive(0, idx)
            for peer in x_peers:
                send(0, idx, peer)
        for x in x_others:
            idx = block(z, y_me, x)
            arrive(1, idx)
            for peer in y_peers:
                send(1, idx, peer)

    stages = [[] for _ in range(groups)]
    tasks = [near_plane]
    tasks += [functools.partial(far_column, z) for z in z_others]
    tasks += [functools.partial(far_plane, z) for z in z_others]
    for i, task in enumerate(tasks):
        stages[min(i * groups // len(tasks), groups - 1)].append(task)

    tq_copy.wait()
    for h in range(heads):
        cols = slice(h * size, (h + 1) * size)
        text = tq_buf[:, cols].astype(jnp.float32)
        text = text * rsqrt_mean(text) * tqg_ref[...]
        image = turned(iq_ref[:, cols].astype(jnp.float32), iqg_ref[...])
        qs[h] = jnp.concatenate([text, image], axis=0).astype(jnp.bfloat16)

    valid = lax.broadcasted_iota(jnp.int32, (rows, text_rows), 1) < length_ref[0]

    def scores_of(query, key):
        return (
            lax.dot_general(
                query, key, (((1,), (1,)), ((), ())), preferred_element_type=jnp.float32
            )
            * scale
        )

    for g in range(groups):
        for copy in text_copies[g]:
            copy.wait()
        for i in range(per):
            h = g * per + i
            cols = slice(i * size, (i + 1) * size)
            key = tk_buf[g, :, cols].astype(jnp.float32)
            key = (key * rsqrt_mean(key) * tkg_ref[...]).astype(jnp.bfloat16)
            scores = jnp.where(valid, scores_of(qs[h], key), LOW)
            top = jnp.max(scores, axis=-1, keepdims=True)
            expo = jnp.where(valid, jnp.exp2(scores - top), 0.0)
            m_buf[h] = jnp.broadcast_to(top, (rows, size))
            l_buf[h] = jnp.broadcast_to(jnp.sum(expo, axis=-1, keepdims=True), (rows, size))
            o_buf[h] = jnp.dot(
                expo.astype(jnp.bfloat16),
                tv_buf[g, :, cols],
                preferred_element_type=jnp.float32,
            )
        for task in stages[g]:
            task()

    for z in [z_me] + z_others:
        for y in [y_me] + y_others:
            for x in x_others:
                arrive(0, block(z, y, x))
        for x in [x_me] + x_others:
            for y in y_others:
                arrive(1, block(z, y, x))

    for h in range(heads):
        cols = slice(h * size, (h + 1) * size)
        key = kbuf[:, :, cols].astype(jnp.float32).reshape(devices * own_rows, size)
        value = vbuf[:, :, cols].astype(jnp.float32).reshape(devices * own_rows, size)
        scores = scores_of(qs[h], key.astype(jnp.bfloat16))
        old = m_buf[h][:, :1]
        top = jnp.maximum(old, jnp.max(scores, axis=-1, keepdims=True))
        expo = jnp.exp2(scores - top)
        back = jnp.exp2(old - top)
        total = l_buf[h][:, :1] * back + jnp.sum(expo, axis=-1, keepdims=True)
        out = o_buf[h] * back + jnp.dot(
            expo.astype(jnp.bfloat16),
            value.astype(jnp.bfloat16),
            preferred_element_type=jnp.float32,
        )
        out = out / total
        to_ref[:, cols] = out[:share].astype(jnp.bfloat16)
        io_ref[:, cols] = out[share:].astype(jnp.bfloat16)

    for copy in sends:
        copy.wait_send()


def send_count(devices):
    zs, ys, xs = line_sizes(devices)
    keys = (zs - 1) + zs * (ys - 1) + zs * ys * (xs - 1)
    values = (zs - 1) + zs * (xs - 1) + zs * xs * (ys - 1)
    return keys + values


def local(iq, ik, iv, tq, tk, tv, iqg, ikg, tqg, tkg, order, length):
    devices = lax.axis_size("seq")
    own_rows, width = iq.shape
    size = iqg.shape[0]
    heads = width // size
    text_rows = tq.shape[0]
    share = text_rows // devices
    rows = share + own_rows
    groups = heads // 2 if heads % 2 == 0 else heads
    span = width // groups
    vmem = pl.BlockSpec(memory_space=pltpu.VMEM)
    smem = pl.BlockSpec(memory_space=pltpu.SMEM)
    hbm = pl.BlockSpec(memory_space=pl.ANY)
    gains = [g.reshape(1, size) for g in (iqg, ikg, tqg, tkg)]
    return pl.pallas_call(
        functools.partial(kernel, devices),
        out_shape=(
            jax.ShapeDtypeStruct((own_rows, width), jnp.bfloat16),
            jax.ShapeDtypeStruct((share, width), jnp.bfloat16),
        ),
        in_specs=[vmem] * 3 + [hbm] * 3 + [vmem] * 4 + [smem] * 2,
        out_specs=(vmem, vmem),
        scratch_shapes=[
            pltpu.VMEM((devices, own_rows, width), jnp.bfloat16),
            pltpu.VMEM((devices, own_rows, width), jnp.bfloat16),
            pltpu.VMEM((share, width), jnp.bfloat16),
            pltpu.VMEM((groups, text_rows, span), jnp.bfloat16),
            pltpu.VMEM((groups, text_rows, span), jnp.bfloat16),
            pltpu.VMEM((heads, rows, size), jnp.bfloat16),
            pltpu.VMEM((heads, rows, size), jnp.float32),
            pltpu.VMEM((heads, rows, size), jnp.float32),
            pltpu.VMEM((heads, rows, size), jnp.float32),
            pltpu.SemaphoreType.DMA((2, devices)),
            pltpu.SemaphoreType.DMA((send_count(devices),)),
            pltpu.SemaphoreType.DMA((2 * groups + 1,)),
        ],
        compiler_params=pltpu.CompilerParams(
            collective_id=0, has_side_effects=True, vmem_limit_bytes=62 * 1024 * 1024
        ),
    )(iq, ik, iv, tq, tk, tv, *gains, order, length)


def solution(mesh):
    rows = P(("req", "seq"), None)
    text = P("req", None)
    return jax.shard_map(
        local,
        mesh=mesh,
        in_specs=(rows, rows, rows, text, text, text)
        + (P(), P(), P(), P(), P(("req", "seq")), P("req")),
        out_specs=(rows, rows),
        check_vma=False,
    )
```

time: 65.3 us -> 28 us (0.43)
  waiting for transfers between devices: 27.7 us -> 0 us
  Pallas kernels: 0 us -> 23.6 us
  starting transfers between devices: 14 us -> 0 us
  other arithmetic: 8.71 us -> 0 us
  local copies, waits for them, and re-layouts: 9.5 us -> 2.89 us
  matrix products: 2.9 us -> 0 us
  between operations: 1.97 us -> 1.29 us
    ppermute x14 -> x0, waiting for transfers between devices: 27.7 us -> none  [the longest x8 14.3 us: from_partner(): return lax.ppermute(block, axis, route)]
    pallas_call x0 -> x1, Pallas kernels: none -> 23.6 us  [local(): pl.pallas_call(functools.partial(kernel, devices), out_shape=(jax.ShapeDt...]
    ppermute x14 -> x0, starting transfers between devices: 14 us -> none  [the longest x8 9 us: from_partner(): return lax.ppermute(block, axis, route)]
    mul x4 -> x0, other arithmetic: 5.07 us -> none  [the longest x1 3.16 us: rotate(): odd_part * sine_part]
    dot_general x10 -> x0, matrix products: 2.9 us -> none  [the longest x5 1.64 us: partial_attend(): jnp.einsum('rhs,shd->rhd', expo.astype(jnp.bfloat16), value_block.reshape...]
    mul x14 -> x0, local copies, waits for them, and re-layouts: 2.38 us -> none  [the longest x2 0.49 us: rotate(): odd_part * sine_part]
    convert_element_type x5 -> x0, local copies, waits for them, and re-layouts: 2.16 us -> none  [the longest x2 1.81 us: head_norm(): shaped = values.astype(jnp.float32).reshape(row_count, head_count, -1)]
    reduce_sum x9 -> x0, other arithmetic: 1.68 us -> none  [the longest x4 1.12 us: head_norm(): mean_square = jnp.mean(shaped * shaped, axis=-1, keepdims=True)]
  transfers between devices with their start and end apart: 14 -> 0, of which waited for: 9 -> 0; matrix products, arithmetic and copies ran while one was open for 7% -> 0% of each run, Pallas kernels for 0% -> 0%
where the time goes in v1:
time: 28 us; the launch traced here: 27.7 us
  Pallas kernels  23.6 us (84%)
  local copies, waits for them, and re-layouts  2.89 us (10%)
  between operations  1.29 us (5%)
    pallas_call x1, Pallas kernels, local(): pl.pallas_call(functools.partial(kernel, devices), out_shape=(jax.ShapeDt...  23.6 us
    unnamed x2, local copies, waits for them, and re-layouts  2.89 us

profile of v1, /device:TPU:0, one launch (start us, length us, event | category | flops | bytes accessed | tf_op | source)
XLA Modules:
  0.0 27.7 jit_solution(4137613386184919460)
XLA Ops:
  1.3 23.6 %shard_map.131 = (bf16[8,1536]{1,0:T(8,128)(2,1)}, bf16[32,1536]{1,0:T(8,128)(2,1)}) custom-call(bf16[8,1536]{1,0:T(8,128)(2,1)} %iq_ref.1, bf16[8,1536]{1,0:T(8,128)(2,1)} %ik_ref.1, bf16[8,1536]{1,0:T(8,128)(2,1)} %iv_ref.1, bf16[512,1536]{1,0:T(8,128)(2,1)} %tq_ref.1, bf16[512,1536]{1,0:T(8,128)(2,1)} %tk_ref.1, bf16[512,1536]{1,0:T(8,128)(2,1)} %tv_ref.1, ...), custom_call_target="tpu_custom_call" | custom-call | tf_op jit(solution)/shard_map/pallas_call | solution.py:316
  24.8 1.3 %copy.17 = bf16[8,1536]{1,0:T(8,128)(2,1)} copy(bf16[8,1536]{1,0:T(8,128)(2,1)} %get-tuple-element.4) | data formatting | bytes 49152
  26.2 1.5 %copy.18 = bf16[32,1536]{1,0:T(8,128)(2,1)} copy(bf16[32,1536]{1,0:T(8,128)(2,1)} %get-tuple-element.5) | data formatting | bytes 196608

commit v2 on v1

--- a/solution.py
+++ b/solution.py
@@ -269,24 +269,35 @@
             for y in y_others:
                 arrive(1, block(z, y, x))
 
-    for h in range(heads):
-        cols = slice(h * size, (h + 1) * size)
-        key = kbuf[:, :, cols].astype(jnp.float32).reshape(devices * own_rows, size)
-        value = vbuf[:, :, cols].astype(jnp.float32).reshape(devices * own_rows, size)
-        scores = scores_of(qs[h], key.astype(jnp.bfloat16))
-        old = m_buf[h][:, :1]
-        top = jnp.maximum(old, jnp.max(scores, axis=-1, keepdims=True))
-        expo = jnp.exp2(scores - top)
-        back = jnp.exp2(old - top)
-        total = l_buf[h][:, :1] * back + jnp.sum(expo, axis=-1, keepdims=True)
-        out = o_buf[h] * back + jnp.dot(
-            expo.astype(jnp.bfloat16),
-            value.astype(jnp.bfloat16),
+    def lanes(h):
+        return slice(h * size, (h + 1) * size)
+
+    def gathered(buf, h):
+        whole = buf[:, :, lanes(h)].astype(jnp.float32)
+        return whole.reshape(devices * own_rows, size).astype(jnp.bfloat16)
+
+    every = range(heads)
+    scores = [scores_of(qs[h], gathered(kbuf, h)) for h in every]
+    olds = [m_buf[h] for h in every]
+    tops = [
+        jnp.maximum(olds[h][:, :1], jnp.max(scores[h], axis=-1, keepdims=True))
+        for h in every
+    ]
+    expos = [jnp.exp2(scores[h] - tops[h]) for h in every]
+    added = [
+        jnp.dot(
+            expos[h].astype(jnp.bfloat16),
+            gathered(vbuf, h),
             preferred_element_type=jnp.float32,
         )
-        out = out / total
-        to_ref[:, cols] = out[:share].astype(jnp.bfloat16)
-        io_ref[:, cols] = out[share:].astype(jnp.bfloat16)
+        for h in every
+    ]
+    sums = [jnp.sum(expos[h], axis=-1, keepdims=True) for h in every]
+    for h in every:
+        back = jnp.exp2(olds[h] - tops[h])
+        out = (o_buf[h] * back + added[h]) / (l_buf[h] * back + sums[h])
+        to_ref[:, lanes(h)] = out[:share].astype(jnp.bfloat16)
+        io_ref[:, lanes(h)] = out[share:].astype(jnp.bfloat16)
 
     for copy in sends:
         copy.wait_send()

time: 28 us -> 24.9 us (0.89)
  Pallas kernels: 23.6 us -> 20.5 us
    pallas_call x1, Pallas kernels: 23.6 us -> 20.5 us  [local(): pl.pallas_call(functools.partial(kernel, devices), out_shape=(jax.ShapeDt...]
where the time goes in v2:
time: 24.9 us; the launch traced here: 24.7 us
  Pallas kernels  20.5 us (82%)
  local copies, waits for them, and re-layouts  2.89 us (12%)
  between operations  1.29 us (5%)
    pallas_call x1, Pallas kernels, local(): pl.pallas_call(functools.partial(kernel, devices), out_shape=(jax.ShapeDt...  20.5 us
    unnamed x2, local copies, waits for them, and re-layouts  2.89 us

profile of v2, /device:TPU:0, one launch (start us, length us, event | category | flops | bytes accessed | tf_op | source)
XLA Modules:
  0.0 24.7 jit_solution(7121149123985609131)
XLA Ops:
  1.3 20.5 %shard_map.131 = (bf16[8,1536]{1,0:T(8,128)(2,1)}, bf16[32,1536]{1,0:T(8,128)(2,1)}) custom-call(bf16[8,1536]{1,0:T(8,128)(2,1)} %iq_ref.1, bf16[8,1536]{1,0:T(8,128)(2,1)} %ik_ref.1, bf16[8,1536]{1,0:T(8,128)(2,1)} %iv_ref.1, bf16[512,1536]{1,0:T(8,128)(2,1)} %tq_ref.1, bf16[512,1536]{1,0:T(8,128)(2,1)} %tk_ref.1, bf16[512,1536]{1,0:T(8,128)(2,1)} %tv_ref.1, ...), custom_call_target="tpu_custom_call" | custom-call | tf_op jit(solution)/shard_map/pallas_call | solution.py:327
  21.8 1.3 %copy.17 = bf16[8,1536]{1,0:T(8,128)(2,1)} copy(bf16[8,1536]{1,0:T(8,128)(2,1)} %get-tuple-element.4) | data formatting | bytes 49152
  23.1 1.5 %copy.18 = bf16[32,1536]{1,0:T(8,128)(2,1)} copy(bf16[32,1536]{1,0:T(8,128)(2,1)} %get-tuple-element.5) | data formatting | bytes 196608

commit v3 on v2

--- a/solution.py
+++ b/solution.py
@@ -143,10 +143,19 @@
         )
         return normed * cosine + swapped * sine
 
+    raw = [
+        ik_ref[:, h * size : (h + 1) * size].astype(jnp.float32) for h in range(heads)
+    ]
+    inverse = [rsqrt_mean(part) for part in raw]
+    normed = [part * inv * ikg_ref[...] for part, inv in zip(raw, inverse)]
+    right = [pltpu.roll(part, size - 1, 1) for part in normed]
+    left = [pltpu.roll(part, 1, 1) for part in normed]
+    keys = [
+        part * cosine + jnp.where(even, r, l) * sine
+        for part, r, l in zip(normed, right, left)
+    ]
     for h in range(heads):
-        cols = slice(h * size, (h + 1) * size)
-        key = turned(ik_ref[:, cols].astype(jnp.float32), ikg_ref[...])
-        kbuf[me, :, cols] = key.astype(jnp.bfloat16)
+        kbuf[me, :, h * size : (h + 1) * size] = keys[h].astype(jnp.bfloat16)
     vbuf[me] = iv_ref[...]
 
     pl.semaphore_wait(barrier, len(peers))

time: 24.9 us -> 25 us (level)
  no operation moved by 1% of the time
where the time goes in v3:
time: 25 us; the launch traced here: 24.7 us
  Pallas kernels  20.5 us (82%)
  local copies, waits for them, and re-layouts  2.89 us (12%)
  between operations  1.29 us (5%)
    pallas_call x1, Pallas kernels, local(): pl.pallas_call(functools.partial(kernel, devices), out_shape=(jax.ShapeDt...  20.5 us
    unnamed x2, local copies, waits for them, and re-layouts  2.89 us

profile of v3, /device:TPU:0, one launch (start us, length us, event | category | flops | bytes accessed | tf_op | source)
XLA Modules:
  0.0 24.7 jit_solution(18304112056642138737)
XLA Ops:
  1.3 20.5 %shard_map.131 = (bf16[8,1536]{1,0:T(8,128)(2,1)}, bf16[32,1536]{1,0:T(8,128)(2,1)}) custom-call(bf16[8,1536]{1,0:T(8,128)(2,1)} %iq_ref.1, bf16[8,1536]{1,0:T(8,128)(2,1)} %ik_ref.1, bf16[8,1536]{1,0:T(8,128)(2,1)} %iv_ref.1, bf16[512,1536]{1,0:T(8,128)(2,1)} %tq_ref.1, bf16[512,1536]{1,0:T(8,128)(2,1)} %tk_ref.1, bf16[512,1536]{1,0:T(8,128)(2,1)} %tv_ref.1, ...), custom_call_target="tpu_custom_call" | custom-call | tf_op jit(solution)/shard_map/pallas_call | solution.py:336
  21.8 1.3 %copy.17 = bf16[8,1536]{1,0:T(8,128)(2,1)} copy(bf16[8,1536]{1,0:T(8,128)(2,1)} %get-tuple-element.4) | data formatting | bytes 49152
  23.2 1.5 %copy.18 = bf16[32,1536]{1,0:T(8,128)(2,1)} copy(bf16[32,1536]{1,0:T(8,128)(2,1)} %get-tuple-element.5) | data formatting | bytes 196608
